TPU v7x, 32 devices: a whole 2x2x4 slice. The times are simulated.
32 devices in a mesh: tm: 8 (over z, y), group: 4 (over x, core).
Axes of the slice: x: 2, y: 2, z: 4, core: 2. Of those that a mesh axis runs over, the one named last changes fastest.
Arguments:
- values: float32 [65536, 64], P(('tm', 'group')), may hold values from -6 to 6
- group_ids: int32 [65536], P(('tm', 'group')), may hold values from 0 to 2047, as said below
- slot_of: int32 [2048], replicated, may hold values from 0 to 2047, each once
Outputs:
- running_mean: float32 [65536, 64], P(('tm', 'group'))
- running_count: int32 [65536], P(('tm', 'group'))
- closing_mean: float32 [2048, 64], P('group')
Inputs may be any that keep to these rules, and one draw needn't show every extreme that they name: `slot_of`: a permutation of the slots; slot s belongs to index s // (2048 / 4) of the group axis. `group_ids`: some store groups may have no rows in the window.
All inputs are finite; a program needn't handle non-finite values.
Results may differ from a plain program's by a relative error of at most 0.0003.
Values sent between devices are 32-bit elements; how exact they have to be, the bound alone decides.
A program may use at most 64 MiB of HBM per device.

v0:
```python
import math

import jax
import jax.numpy as jnp
from jax import lax
from jax.sharding import PartitionSpec as P


def carried_in(shard, axis, combine, identity):
    devices, mine = (lax.axis_size(axis), lax.axis_index(axis))
    everything = jax.tree.map(lambda part: lax.all_gather(part, axis), shard)
    start = jax.tree.map(
        lambda part, zero: jnp.broadcast_to(jnp.asarray(zero, part.dtype), part.shape),
        shard,
        identity,
    )

    def step(k, before):
        reached = k < mine
        new = combine(before, jax.tree.map(lambda part: part[k], everything))
        return jax.tree.map(lambda a, b: jnp.where(reached, a, b), new, before)

    return lax.fori_loop(0, devices, step, start)


def block_totals(values, slots, groups):
    total_rows, width = values.shape
    size = math.gcd(total_rows, 512)
    blocks = total_rows // size
    labels = jnp.arange(groups, dtype=jnp.int32)

    def collect(carry, item):
        rows, keys = item
        onehot = (keys[:, None] == labels[None, :]).astype(jnp.float32)
        sums = lax.dot_general(
            onehot,
            rows,
            (((0,), (0,)), ((), ())),
            precision=lax.Precision.HIGHEST,
            preferred_element_type=jnp.float32,
        )
        return (carry, (sums, jnp.sum(onehot, axis=0)))

    _, stacked = lax.scan(
        collect,
        jnp.zeros((), jnp.float32),
        (values.reshape(blocks, size, width), slots.reshape(blocks, size)),
    )
    return (stacked[0], stacked[1])


def running_pass(values, slots, sums, counts, block_sums, block_counts):
    total_rows, width = values.shape
    blocks = block_sums.shape[0]
    size = total_rows // blocks
    lower = jnp.arange(size)[:, None] >= jnp.arange(size)[None, :]

    def advance(carry, item):
        state, tallies = carry
        rows, keys, add_sums, add_counts = item
        mask = ((keys[:, None] == keys[None, :]) & lower).astype(jnp.float32)
        within = jnp.dot(
            mask, rows, precision=lax.Precision.HIGHEST, preferred_element_type=jnp.float32
        )
        inclusive = within + jnp.take(state, keys, axis=0)
        tally = jnp.sum(mask, axis=1) + jnp.take(tallies, keys)
        return ((state + add_sums, tallies + add_counts), (inclusive, tally))

    items = (
        values.reshape(blocks, size, width),
        slots.reshape(blocks, size),
        block_sums,
        block_counts,
    )
    _, outs = lax.scan(advance, (sums, counts), items)
    return (outs[0].reshape(total_rows, width), outs[1].reshape(total_rows))


def add_pair(earlier, later):
    return (earlier[0] + later[0], earlier[1] + later[1])


def carries(local_sums, local_counts):
    groups, width = local_sums.shape
    owners = lax.axis_size("group")
    per_owner = groups // owners
    zero_block = (jnp.zeros((per_owner, width), jnp.float32), jnp.zeros((per_owner,), jnp.float32))
    arrived_sums, arrived_counts = (
        lax.all_to_all(
            local_sums.reshape(owners, per_owner, width),
            "group",
            split_axis=0,
            concat_axis=0,
            tiled=True,
        ),
        lax.all_to_all(
            local_counts.reshape(owners, per_owner),
            "group",
            split_axis=0,
            concat_axis=0,
            tiled=True,
        ),
    )
    slice_sums = jnp.sum(arrived_sums, axis=0)
    slice_counts = jnp.sum(arrived_counts, axis=0)
    inner_sums = jnp.cumsum(arrived_sums, axis=0) - arrived_sums
    inner_counts = jnp.cumsum(arrived_counts, axis=0) - arrived_counts
    chain_sums, chain_counts = carried_in((slice_sums, slice_counts), "tm", add_pair, zero_block)
    closing_sums, closing_counts = lax.psum((slice_sums, slice_counts), "tm")
    back_sums, back_counts = (
        lax.all_to_all(
            chain_sums[None] + inner_sums, "group", split_axis=0, concat_axis=0, tiled=True
        ),
        lax.all_to_all(
            chain_counts[None] + inner_counts, "group", split_axis=0, concat_axis=0, tiled=True
        ),
    )
    start_sums = back_sums.reshape(groups, width)
    start_counts = back_counts.reshape(groups)
    return (start_sums, start_counts, closing_sums, closing_counts)


def local(values, group_ids, slot_of):
    groups = slot_of.shape[0]
    width = values.shape[1]
    slots = jnp.take(slot_of, group_ids)
    block_sums, block_counts = block_totals(values, slots, groups)
    local_sums = jnp.sum(block_sums, axis=0)
    local_counts = jnp.sum(block_counts, axis=0)
    empty_sums = jnp.zeros((groups, width), jnp.float32)
    empty_counts = jnp.zeros((groups,), jnp.float32)
    own_sum, own_count = running_pass(
        values, slots, empty_sums, empty_counts, block_sums, block_counts
    )
    start_sums, start_counts, closing_sums, closing_counts = carries(local_sums, local_counts)
    running_sum = own_sum + jnp.take(start_sums, slots, axis=0)
    count = own_count + jnp.take(start_counts, slots)
    running_mean = running_sum / count[:, None]
    closing_mean = closing_sums / jnp.maximum(closing_counts, 1.0)[:, None]
    return (running_mean, count.astype(jnp.int32), closing_mean)


def solution(mesh):
    in_specs = (P(("tm", "group"), None), P(("tm", "group")), P())
    out_specs = (P(("tm", "group"), None), P(("tm", "group")), P("group", None))
    return jax.shard_map(local, mesh=mesh, in_specs=in_specs, out_specs=out_specs, check_vma=False)
```

profile of v0, /device:TPU:0, one launch (start us, length us, event | category | flops | bytes accessed | tf_op | source)
XLA Modules:
  0.0 227.2 jit_solution(1361855397270004344)
XLA Ops:
  7.9 11.8 %gather_fusion.2 = s32[2048]{0:T(1024)S(1)} fusion(s32[2048]{0:T(1024)S(1)} %copy-done, s32[2048]{0:T(1024)S(1)} %fusion.26), kind=kCustom, calls=%fused_computation.2 | custom fusion | bytes 24576 | tf_op jit(solution)/shard_map/jit(_take)/gather | solution.py:126
  20.1 13.2 %while.46 = (s32[]{:T(128)}, f32[4,2048,64]{1,2,0:T(8,128)}, f32[4,2048]{1,0:T(4,128)S(1)}, s32[4,512]{1,0:T(4,128)S(1)}, f32[4,512,64]{2,1,0:T(8,128)S(1)}, /*index=5*/s32[]{:T(128)}, s32[]{:T(128)}) while((s32[]{:T(128)}, f32[4,2048,64]{1,2,0:T(8,128)}, f32[4,2048]{1,0:T(4,128)S(1)}, s32[4,512]{1,0:T(4,128)S(1)}, ...), condition=%wide.region_2.3_spmd.clone, body=%wide.region_0.0_spmd.clone.sunk | while | flops 809498624 | bytes 820317 | solution.py:44
  20.1 2.6 %fusion.41 = f32[4,2048,64]{1,2,0:T(8,128)} fusion(f32[4,2048,64]{1,2,0:T(8,128)} %get-tuple-element.536, s32[]{:T(128)S(6)} %copy.70, s32[512]{0:T(512)S(1)} %bitcast.93, f32[4,512,64]{2,1,0:T(8,128)S(1)} %get-tuple-element.546), kind=kOutput, calls=%fused_computation.12.clone.1 | convolution fusion | flops 806354944 | bytes 789504 | tf_op jit(solution)/shard_map/while/body/eval_jaxpr/dot_general | solution.py:35
  23.4 2.6 %fusion.41 = f32[4,2048,64]{1,2,0:T(8,128)} fusion(f32[4,2048,64]{1,2,0:T(8,128)} %get-tuple-element.536, s32[]{:T(128)S(6)} %copy.70, s32[512]{0:T(512)S(1)} %bitcast.93, f32[4,512,64]{2,1,0:T(8,128)S(1)} %get-tuple-element.546), kind=kOutput, calls=%fused_computation.12.clone.1 | convolution fusion | flops 806354944 | bytes 789504 | tf_op jit(solution)/shard_map/while/body/eval_jaxpr/dot_general | solution.py:35
  26.7 2.6 %fusion.41 = f32[4,2048,64]{1,2,0:T(8,128)} fusion(f32[4,2048,64]{1,2,0:T(8,128)} %get-tuple-element.536, s32[]{:T(128)S(6)} %copy.70, s32[512]{0:T(512)S(1)} %bitcast.93, f32[4,512,64]{2,1,0:T(8,128)S(1)} %get-tuple-element.546), kind=kOutput, calls=%fused_computation.12.clone.1 | convolution fusion | flops 806354944 | bytes 789504 | tf_op jit(solution)/shard_map/while/body/eval_jaxpr/dot_general | solution.py:35
  30.0 2.6 %fusion.41 = f32[4,2048,64]{1,2,0:T(8,128)} fusion(f32[4,2048,64]{1,2,0:T(8,128)} %get-tuple-element.536, s32[]{:T(128)S(6)} %copy.70, s32[512]{0:T(512)S(1)} %bitcast.93, f32[4,512,64]{2,1,0:T(8,128)S(1)} %get-tuple-element.546), kind=kOutput, calls=%fused_computation.12.clone.1 | convolution fusion | flops 806354944 | bytes 789504 | tf_op jit(solution)/shard_map/while/body/eval_jaxpr/dot_general | solution.py:35
  33.3 1.0 copy-done.3
  34.3 1.8 reduce_sum.56
  36.9 4.2 %all-to-all-start = ((f32[4,512,64]{1,2,0:T(8,128)}), f32[4,512,64]{1,2,0:T(8,128)S(1)}, u32[]{:S(2)}, u32[]{:S(2)}) async-start(f32[4,512,64]{1,2,0:T(8,128)} %bitcast.47), calls=%async_computation | async-start | bytes 1048576 | tf_op jit(solution)/shard_map/all_to_all | solution.py:89
  41.8 8.2 %all-to-all-done = f32[4,512,64]{1,2,0:T(8,128)S(1)} async-done(((f32[4,512,64]{1,2,0:T(8,128)}), f32[4,512,64]{1,2,0:T(8,128)S(1)}, u32[]{:S(2)}, u32[]{:S(2)}) %all-to-all-start) | async-done | bytes 524320 | tf_op jit(solution)/shard_map/all_to_all | solution.py:89
  50.0 3.2 %all-to-all-start.1 = ((f32[4,1,512]{2,1,0:T(1,128)}), f32[4,1,512]{2,1,0:T(1,128)S(1)}, u32[]{:S(2)}, u32[]{:S(2)}) async-start(f32[4,1,512]{2,1,0:T(1,128)} %bitcast.3), calls=%async_computation.1 | async-start | bytes 16384 | tf_op jit(solution)/shard_map/all_to_all | solution.py:96
  54.2 34.8 %while.47 = (s32[]{:T(128)}, f32[2048,64]{1,0:T(8,128)S(1)}, f32[2048]{0:T(1024)S(1)}, f32[4,512,64]{1,2,0:T(8,128)}, f32[4,512]{1,0:T(4,128)S(1)}, /*index=5*/f...) while((s32[]{:T(128)}, f32[2048,64]{1,0:T(8,128)S(1)}, ...), condition=%wide.region_5.6_spmd.clone, body=%wide.region_3.5_spmd.clone.sunk | while | flops 203764736 | bytes 5337232 | solution.py:75
  54.2 1.1 constant_dynamic-slice_fusion.11
  56.0 1.0 gather_fusion
  57.2 2.3 fusion.46
  59.7 3.1 %gather_fusion.1 = f32[512]{0:T(512)S(1)} fusion(f32[2048]{0:T(1024)S(1)} %get-tuple-element.521, s32[1024]{0:T(1024)S(1)} %pad_clamp_fusion.2), kind=kCustom, calls=%fused_computation.1.clone.clone.1 | custom fusion | bytes 6144 | tf_op jit(solution)/shard_map/while/body/eval_jaxpr/jit(_take)/gather | solution.py:66
  62.9 1.1 constant_dynamic-slice_fusion.11
  64.7 1.0 gather_fusion
  65.9 2.3 %fusion.46 = f32[4,512,64]{1,2,0:T(8,128)} fusion(f32[4,512,64]{1,2,0:T(8,128)} %get-tuple-element.563, s32[]{:T(128)S(6)} %copy.81, s32[512]{0:T(512)S(1)} %bitcast.83, f32[4,512,64]{2,1,0:T(8,128)} %get-tuple-element.579, f32[512,64]{0,1:T(8,128)S(1)} %copy.62, pred[512]{0:T(512)(128)(4,1)S(1)} %compare_and_fusion.4), kind=kOutput, calls=%fused_computation.20.clone.1 | convolution fusion | flops 202178560 | bytes 529920 | tf_op jit(solution)/shard_map/while/body/eval_jaxpr/dot_general | solution.py:62
  68.4 3.1 %gather_fusion.1 = f32[512]{0:T(512)S(1)} fusion(f32[2048]{0:T(1024)S(1)} %get-tuple-element.521, s32[1024]{0:T(1024)S(1)} %pad_clamp_fusion.2), kind=kCustom, calls=%fused_computation.1.clone.clone.1 | custom fusion | bytes 6144 | tf_op jit(solution)/shard_map/while/body/eval_jaxpr/jit(_take)/gather | solution.py:66
  71.6 1.1 constant_dynamic-slice_fusion.11
  73.4 1.0 gather_fusion
  74.6 2.3 fusion.46
  77.1 3.1 %gather_fusion.1 = f32[512]{0:T(512)S(1)} fusion(f32[2048]{0:T(1024)S(1)} %get-tuple-element.521, s32[1024]{0:T(1024)S(1)} %pad_clamp_fusion.2), kind=kCustom, calls=%fused_computation.1.clone.clone.1 | custom fusion | bytes 6144 | tf_op jit(solution)/shard_map/while/body/eval_jaxpr/jit(_take)/gather | solution.py:66
  80.3 1.1 constant_dynamic-slice_fusion.11
  82.1 1.0 gather_fusion
  83.3 2.3 fusion.46
  85.8 3.1 %gather_fusion.1 = f32[512]{0:T(512)S(1)} fusion(f32[2048]{0:T(1024)S(1)} %get-tuple-element.521, s32[1024]{0:T(1024)S(1)} %pad_clamp_fusion.2), kind=kCustom, calls=%fused_computation.1.clone.clone.1 | custom fusion | bytes 6144 | tf_op jit(solution)/shard_map/while/body/eval_jaxpr/jit(_take)/gather | solution.py:66
  89.1 1.4 copy.41
  90.5 27.5 %all-gather.2 = f32[8,1,512]{2,1,0:T(1,128)S(1)} all-gather(f32[1,1,512]{2,1,0:T(1,128)S(1)} %bitcast.97), channel_id=3, replica_groups=mesh['tm'=8,'group'=4] {'tm'}, dimensions={0}, use_global_device_ids=true | all-gather | bytes 18432 | tf_op jit(solution)/shard_map/all_gather | solution.py:11
  118.0 19.8 %psum.15 = f32[512]{0:T(512)S(1)} all-reduce(f32[512]{0:T(512)S(1)} %reduce_sum.59), channel_id=1, replica_groups=mesh['tm'=8,'group'=4] {'tm'}, use_global_device_ids=true, to_apply=%region_15.16 | all-reduce | flops 512 | bytes 4096 | tf_op jit(solution)/shard_map/psum | solution.py:109
  138.5 8.7 %while.48 = (s32[]{:T(128)}, f32[512,64]{1,0:T(8,128)S(1)}, f32[512]{0:T(512)S(1)}, s32[]{:T(128)}, f32[8,512,64]{2,1,0:T(8,128)}, /*index=5*/f32[8,512]{1,0:T(8,128)S(1)}, s32[]{:T(128)}, s32[]{:T(128)}) while((s32[]{:T(128)}, f32[512,64]{1,0:T(8,128)S(1)}, f32[512]{0:T(512)S(1)}, s32[]{:T(128)}, f32[8,512,64]{2,1,0:T(8,128)}, ...), condition=%wide.region_11.12_spmd.clone, body=%wide.region_10.11_spmd.clone.sunk | while | flops 99844 | bytes 403579 | solution.py:23
  138.5 1.1 add_select_fusion.4
  139.7 1.0 add_select_fusion.4
  140.8 1.0 add_select_fusion.4
  141.9 1.0 add_select_fusion.4
  142.9 1.0 add_select_fusion.4
  144.0 1.0 add_select_fusion.4
  145.1 1.0 add_select_fusion.4
  146.2 1.0 add_select_fusion.4
  148.0 3.2 %all-to-all-start.3 = ((f32[4,1,512]{2,1,0:T(1,128)}), f32[4,1,512]{2,1,0:T(1,128)S(1)}, u32[]{:S(2)}, u32[]{:S(2)}) async-start(f32[4,1,512]{2,1,0:T(1,128)} %fusion.24), calls=%async_computation.3 | async-start | bytes 16384 | tf_op jit(solution)/shard_map/all_to_all | solution.py:114
  152.1 2.9 %all-to-all-done.3 = f32[4,1,512]{2,1,0:T(1,128)S(1)} async-done(((f32[4,1,512]{2,1,0:T(1,128)}), f32[4,1,512]{2,1,0:T(1,128)S(1)}, u32[]{:S(2)}, u32[]{:S(2)}) %all-to-all-start.3) | async-done | bytes 8224 | tf_op jit(solution)/shard_map/all_to_all | solution.py:114
  155.0 3.5 %all-to-all-start.2 = ((f32[4,512,64]{1,2,0:T(8,128)}), f32[4,512,64]{1,2,0:T(8,128)S(1)}, u32[]{:S(2)}, u32[]{:S(2)}) async-start(f32[4,512,64]{1,2,0:T(8,128)} %fusion.23), calls=%async_computation.2 | async-start | bytes 1048576 | tf_op jit(solution)/shard_map/all_to_all | solution.py:111
  158.5 11.8 %gather_fusion.4 = f32[2048]{0:T(1024)S(1)} fusion(f32[2048]{0:T(1024)S(1)} %bitcast.79, s32[2048]{0:T(1024)S(1)} %get-tuple-element.391), kind=kCustom, calls=%fused_computation.4 | custom fusion | bytes 24576 | tf_op jit(solution)/shard_map/jit(_take)/gather | solution.py:137
  170.9 39.8 %all-reduce.2.cloned.1.call-done = f32[512,64]{1,0:T(8,128)} async-done(((f32[512,64]{1,0:T(8,128)}), f32[512,64]{1,0:T(8,128)}) %all-reduce.2.cloned.1.call-update) | async-done | bytes 131088 | tf_op jit(solution)/shard_map/psum | solution.py:109
  210.7 1.1 broadcast_divide_fusion
  212.9 5.5 %gather_fusion.3 = f32[2048,64]{1,0:T(8,128)S(1)} fusion(f32[2048,64]{1,0:T(8,128)S(1)} %bitcast.80, s32[2048]{0:T(1024)S(1)} %get-tuple-element.391), kind=kCustom, calls=%fused_computation.3 | custom fusion | bytes 1056768 | tf_op jit(solution)/shard_map/jit(_take)/gather | solution.py:136
  219.2 1.1 copy.47
  (117 shorter events, 15.7 us)
Async XLA Ops:
  7.2 0.7 copy-start
  7.9 11.8 %copy-start.5 = (s32[2048]{0:T(1024)S(1)}, s32[2048]{0:T(1024)}, u32[]{:S(2)}) copy-start(s32[2048]{0:T(1024)} %param.10) | copy-start | bytes 24580
  7.9 11.8 %copy-start.4 = (f32[2048,64]{0,1:T(8,128)S(1)}, f32[2048,64]{0,1:T(8,128)}, u32[]{:S(2)}) copy-start(f32[2048,64]{0,1:T(8,128)} %param.9) | copy-start | bytes 1572868
  33.3 1.0 copy-start.3
  36.9 13.0 %all-to-all-start = ((f32[4,512,64]{1,2,0:T(8,128)}), f32[4,512,64]{1,2,0:T(8,128)S(1)}, u32[]{:S(2)}, u32[]{:S(2)}) async-start(f32[4,512,64]{1,2,0:T(8,128)} %bitcast.47), calls=%async_computation | async-start | bytes 1048576 | tf_op jit(solution)/shard_map/all_to_all | solution.py:89
  50.0 4.2 %copy-start.1 = (f32[4,512,64]{1,2,0:T(8,128)}, f32[4,512,64]{1,2,0:T(8,128)S(1)}, u32[]{:S(2)}) copy-start(f32[4,512,64]{1,2,0:T(8,128)S(1)} %all-to-all-done) | copy-start | bytes 1572868
  50.0 40.5 %all-to-all-start.1 = ((f32[4,1,512]{2,1,0:T(1,128)}), f32[4,1,512]{2,1,0:T(1,128)S(1)}, u32[]{:S(2)}, u32[]{:S(2)}) async-start(f32[4,1,512]{2,1,0:T(1,128)} %bitcast.3), calls=%async_computation.1 | async-start | bytes 16384 | tf_op jit(solution)/shard_map/all_to_all | solution.py:96
  53.2 84.5 %all-gather.5.cloned.1.call-start = ((), (), s32[]{:S(2)}) async-start(), calls=%async_computation.5 | async-start | bytes 2359296 | tf_op jit(solution)/shard_map/all_gather | solution.py:11
  137.8 73.0 %all-reduce.2.cloned.1.call-start = ((), (), s32[]{:S(2)}) async-start(), calls=%async_computation.4 | async-start | bytes 524288 | tf_op jit(solution)/shard_map/psum | solution.py:109
  138.5 12.7 %copy-start.2 = (f32[4,512,64]{1,2,0:T(8,128)S(1)}, f32[4,512,64]{1,2,0:T(8,128)}, u32[]{:S(2)}) copy-start(f32[4,512,64]{1,2,0:T(8,128)} %copy-done.1) | copy-start | bytes 1572868
  148.0 7.0 %all-to-all-start.3 = ((f32[4,1,512]{2,1,0:T(1,128)}), f32[4,1,512]{2,1,0:T(1,128)S(1)}, u32[]{:S(2)}, u32[]{:S(2)}) async-start(f32[4,1,512]{2,1,0:T(1,128)} %fusion.24), calls=%async_computation.3 | async-start | bytes 16384 | tf_op jit(solution)/shard_map/all_to_all | solution.py:114
  155.0 57.6 %all-to-all-start.2 = ((f32[4,512,64]{1,2,0:T(8,128)}), f32[4,512,64]{1,2,0:T(8,128)S(1)}, u32[]{:S(2)}, u32[]{:S(2)}) async-start(f32[4,512,64]{1,2,0:T(8,128)} %fusion.23), calls=%async_computation.2 | async-start | bytes 1048576 | tf_op jit(solution)/shard_map/all_to_all | solution.py:111
Sparse Core Ops, SparseCore 0:
  56.2 51.5 all-gather.4
  141.9 68.7 all-reduce.1
where the time goes:
time: 228 us; the launch traced here: 227 us
  local copies, waits for them, and re-layouts  59.4 us (26%)
  waiting for transfers between devices  51.6 us (23%)
  blocking collectives  47.2 us (21%)
  other arithmetic  20.1 us (9%)
  matrix products  19.3 us (8%)
  starting transfers between devices  14.3 us (6%)
  between operations  14.3 us (6%)
    psum x1, waiting for transfers between devices, carries(): closing_sums, closing_counts = lax.psum((slice_sums, slice_counts), 'tm')  39.8 us
    all_gather x1, blocking collectives, carried_in(): everything = jax.tree.map(lambda part: lax.all_gather(part, axis), shard)  27.5 us
    psum x1, blocking collectives, carries(): closing_sums, closing_counts = lax.psum((slice_sums, slice_counts), 'tm')  19.8 us
    gather x4, local copies, waits for them, and re-layouts, advance(): tally = jnp.sum(mask, axis=1) + jnp.take(tallies, keys)  12.6 us
    gather x1, local copies, waits for them, and re-layouts, local(): slots = jnp.take(slot_of, group_ids)  11.8 us
    gather x1, local copies, waits for them, and re-layouts, local(): count = own_count + jnp.take(start_counts, slots)  11.8 us
    dot_general x4, matrix products, collect(): lax.dot_general(onehot, rows, (((0,), (0,)), ((), ())), precision=lax.Pre...  10.3 us
    dot_general x4, matrix products, advance(): jnp.dot(mask, rows, precision=lax.Precision.HIGHEST, preferred_element_ty...  9.06 us
  transfers between devices with their start and end apart: 6, of which 3 were waited for; matrix products, arithmetic and copies ran while one was open for 27% of the time, Pallas kernels for 0%

commit v1 on v0

v1 whole, which is shorter than its diff:
```python
import functools

import jax
import jax.numpy as jnp
from jax import lax
from jax.experimental import pallas as pl
from jax.experimental.pallas import tpu as pltpu
from jax.sharding import PartitionSpec as P

MESH = pl.DeviceIdType.MESH
LANES = 128
ROWS8 = 8
F32 = jnp.float32
BF16 = jnp.bfloat16


def split_parts(x, parts):
    pieces = []
    for _ in range(parts):
        piece = x.astype(BF16).astype(F32)
        pieces.append(piece)
        x = x - piece
    return pieces


def kernel(
    na, nb, ng, count_parts, extra,
    vt_ref, ids_ref, table_ref,
    mean_ref, count_ref, closing_ref,
    lhsv, onehot, acc, lhss, mine, arrived, zbuf, back, start, shut,
    send1, recv1, sendz, recvz, send2, recv2, sendc, recvc,
):
    width, rows = vt_ref.shape
    groups = onehot.shape[0]
    plane = nb * ng
    per = groups // plane
    tm = lax.axis_index("tm")
    g_me = lax.axis_index("group")
    a_me, b_me = tm // nb, tm % nb
    p_me = b_me * ng + g_me
    o_me = g_me * nb + b_me

    def at_position(p):
        return (a_me * nb + p // ng, p % ng)

    def at_owner(o):
        return (a_me * nb + o % nb, o // nb)

    barrier = pltpu.get_barrier_semaphore()
    for k in range(1, plane):
        pl.semaphore_signal(
            barrier, inc=1, device_id=at_position((p_me + k) % plane), device_id_type=MESH
        )
    for k in range(1, na):
        pl.semaphore_signal(
            barrier, inc=1, device_id=(((a_me + k) % na) * nb + b_me, g_me), device_id_type=MESH
        )

    ids = ids_ref[...]
    low, high = ids & (LANES - 1), ids // LANES
    slots = []
    for i in range(0, ids.shape[0], ROWS8):
        index, page = low[i : i + ROWS8], high[i : i + ROWS8]
        found = jnp.zeros_like(index)
        for t in range(table_ref.shape[0]):
            entries = jnp.broadcast_to(table_ref[t : t + 1, :], index.shape)
            got = jnp.take_along_axis(entries, index, axis=1)
            found = jnp.where(page == t, got, found)
        slots.append(found)
    slots = jnp.concatenate(slots, axis=0)

    hi, lo = split_parts(vt_ref[...], 2)
    lhsv[0:width, :] = hi.astype(BF16)
    lhsv[width : 2 * width, :] = lo.astype(BF16)
    tail = jnp.where(lax.broadcasted_iota(jnp.int32, (extra, rows), 0) < ROWS8, 1.0, 0.0)
    lhsv[2 * width :, :] = tail.astype(BF16)

    pl.semaphore_wait(barrier, plane - 1 + na - 1)

    def one_chunk(o):
        base = pl.multiple_of(o * per, per)
        labels = lax.broadcasted_iota(jnp.int32, (per, LANES), 0) + o * per
        for b in range(rows // LANES):
            hit = labels == slots[b : b + 1, :]
            onehot[pl.ds(base, per), b * LANES : (b + 1) * LANES] = jnp.where(
                hit, 1.0, 0.0
            ).astype(BF16)
        sums = lax.dot_general(
            lhsv[...],
            onehot[pl.ds(base, per), :],
            (((1,), (1,)), ((), ())),
            preferred_element_type=F32,
        )
        return jnp.concatenate(
            [
                sums[0:width] + sums[width : 2 * width],
                sums[2 * width : 2 * width + ROWS8],
            ],
            axis=0,
        )

    def copy1(k, o, p):
        return pltpu.make_async_remote_copy(
            src_ref=mine.at[k],
            dst_ref=arrived.at[p],
            send_sem=send1.at[k],
            recv_sem=recv1.at[p],
            device_id=at_owner(o),
            device_id_type=MESH,
        )

    for k in range(1, plane):
        o = (o_me + k) % plane
        mine[k] = one_chunk(o)
        copy1(k, o, p_me).start()
    arrived[p_me] = one_chunk(o_me)

    step = min(rows, 2 * LANES)
    idsf = ids.astype(F32)
    columns = jnp.transpose(idsf)
    for i in range(0, rows, step):
        column = jnp.concatenate(
            [columns[:, (i + j) // LANES : (i + j) // LANES + 1] for j in range(0, step, LANES)],
            axis=0,
        )
        blocks = []
        for j in range(i, rows, LANES):
            hit = column == idsf[j // LANES : j // LANES + 1, :]
            if j < i + step:
                q = lax.broadcasted_iota(jnp.int32, (step, LANES), 0)
                r = lax.broadcasted_iota(jnp.int32, (step, LANES), 1) + (j - i)
                hit = hit & (q <= r)
            blocks.append(jnp.where(hit, 1.0, 0.0).astype(BF16))
        part = jnp.dot(
            lhsv[:, i : i + step], jnp.concatenate(blocks, axis=1), preferred_element_type=F32
        )
        if i == 0:
            acc[...] = part
        else:
            acc[:, i:] += part

    for k in range(1, plane):
        p = (p_me + plane - k) % plane
        copy1(k, o_me, p).wait_recv()
    plane_sum = arrived[0]
    for p in range(1, plane):
        plane_sum = plane_sum + arrived[p]
    zbuf[a_me] = plane_sum

    def copyz(k, a):
        return pltpu.make_async_remote_copy(
            src_ref=zbuf.at[a_me],
            dst_ref=zbuf.at[a],
            send_sem=sendz.at[k],
            recv_sem=recvz.at[a],
            device_id=(((a_me + k) % na) * nb + b_me, g_me),
            device_id_type=MESH,
        )

    for k in range(1, na):
        copyz(k, a_me).start()
    for k in range(1, na):
        copyz(k, (a_me + na - k) % na).wait_recv()
    before = jnp.zeros_like(plane_sum)
    total = jnp.zeros_like(plane_sum)
    for a in range(na):
        one = zbuf[a]
        total = total + one
        before = before + jnp.where(a < a_me, one, 0.0)

    for p in range(plane):
        back[p] = before
        if p < plane - 1:
            before = before + arrived[p]

    def copy2(k, o):
        p = (p_me + k) % plane
        return pltpu.make_async_remote_copy(
            src_ref=back.at[p],
            dst_ref=start.at[o],
            send_sem=send2.at[k],
            recv_sem=recv2.at[o],
            device_id=at_position(p),
            device_id_type=MESH,
        )

    for k in range(1, plane):
        copy2(k, o_me).start()

    shut[b_me] = total[0:width] * (1.0 / jnp.maximum(total[width : width + 1], 1.0))

    def copyc(k, b):
        return pltpu.make_async_remote_copy(
            src_ref=shut.at[b_me],
            dst_ref=shut.at[b],
            send_sem=sendc.at[k],
            recv_sem=recvc.at[b],
            device_id=(a_me * nb + (b_me + k) % nb, g_me),
            device_id_type=MESH,
        )

    for k in range(1, nb):
        copyc(k, b_me).start()

    start[o_me] = back[p_me]
    for k in range(1, plane):
        copy2(k, (o_me + plane - k) % plane).wait_recv()
    for o in range(plane):
        one = start[o]
        counts = split_parts(one[width:], count_parts)
        pad = extra // ROWS8 - count_parts
        counts = counts + [jnp.zeros_like(counts[0])] * pad
        stacked = jnp.concatenate(split_parts(one[0:width], 2) + counts, axis=0)
        lhss[:, o * per : (o + 1) * per] = stacked.astype(BF16)

    wide = min(rows, 4 * LANES)
    for i in range(0, rows, wide):
        whole = acc[:, i : i + wide] + jnp.dot(
            lhss[...], onehot[:, i : i + wide], preferred_element_type=F32
        )
        count = whole[2 * width : 2 * width + 1]
        for j in range(1, count_parts):
            count = count + whole[2 * width + j * ROWS8 : 2 * width + j * ROWS8 + 1]
        mean_ref[:, i : i + wide] = (whole[0:width] + whole[width : 2 * width]) * (1.0 / count)
        count = count.astype(jnp.int32)
        for j in range(0, wide, LANES):
            b = (i + j) // LANES
            count_ref[b : b + 1, :] = count[:, j : j + LANES]

    for k in range(1, nb):
        copyc(k, (b_me + nb - k) % nb).wait_recv()
    for b in range(nb):
        closing_ref[:, b * per : (b + 1) * per] = shut[b]

    for k in range(1, plane):
        copy1(k, (o_me + k) % plane, p_me).wait_send()
        copy2(k, o_me).wait_send()
    for k in range(1, na):
        copyz(k, a_me).wait_send()
    for k in range(1, nb):
        copyc(k, b_me).wait_send()


def inner_parts(parts, owner_slots):
    best = 1
    for n in range(1, parts + 1):
        if n * n <= parts and parts % n == 0 and owner_slots % (n * LANES) == 0:
            best = n
    return best


def solution(mesh):
    tm, ng = mesh.shape["tm"], mesh.shape["group"]

    def local(values, group_ids, slot_of):
        rows, width = values.shape
        groups = slot_of.shape[0]
        nb = inner_parts(tm, groups // ng)
        na = tm // nb
        plane = nb * ng
        per = groups // plane
        count_parts = 2 if rows * tm * ng <= 2**17 else 3
        extra = 2 * ROWS8 if count_parts == 2 else 4 * ROWS8
        tall = 2 * width + extra
        sent = width + ROWS8
        vmem = pl.BlockSpec(memory_space=pltpu.VMEM)
        dma = pltpu.SemaphoreType.DMA
        mean, count, closing = pl.pallas_call(
            functools.partial(kernel, na, nb, ng, count_parts, extra),
            out_shape=(
                jax.ShapeDtypeStruct((width, rows), F32),
                jax.ShapeDtypeStruct((rows // LANES, LANES), jnp.int32),
                jax.ShapeDtypeStruct((width, groups // ng), F32),
            ),
            in_specs=[vmem] * 3,
            out_specs=(vmem,) * 3,
            scratch_shapes=[
                pltpu.VMEM((tall, rows), BF16),
                pltpu.VMEM((groups, rows), BF16),
                pltpu.VMEM((tall, rows), F32),
                pltpu.VMEM((tall, groups), BF16),
                pltpu.VMEM((plane, sent, per), F32),
                pltpu.VMEM((plane, sent, per), F32),
                pltpu.VMEM((na, sent, per), F32),
                pltpu.VMEM((plane, sent, per), F32),
                pltpu.VMEM((plane, sent, per), F32),
                pltpu.VMEM((nb, width, per), F32),
                dma((plane,)), dma((plane,)), dma((na,)), dma((na,)),
                dma((plane,)), dma((plane,)), dma((nb,)), dma((nb,)),
            ],
            compiler_params=pltpu.CompilerParams(
                collective_id=0, has_side_effects=True, vmem_limit_bytes=60 * 1024 * 1024
            ),
            name="running_totals",
        )(
            values.T,
            group_ids.reshape(rows // LANES, LANES),
            slot_of.reshape(groups // LANES, LANES),
        )
        return mean.T, count.reshape(rows), closing.T

    in_specs = (P(("tm", "group"), None), P(("tm", "group")), P())
    out_specs = (P(("tm", "group"), None), P(("tm", "group")), P("group", None))
    return jax.shard_map(local, mesh=mesh, in_specs=in_specs, out_specs=out_specs, check_vma=False)
```

time: 228 us -> 37.8 us (0.17)
  local copies, waits for them, and re-layouts: 59.4 us -> 3.17 us
  waiting for transfers between devices: 51.6 us -> 0 us
  blocking collectives: 47.2 us -> 0 us
  Pallas kernels: 0 us -> 33.7 us
  other arithmetic: 20.1 us -> 0 us
  matrix products: 19.3 us -> 0 us
  starting transfers between devices: 14.3 us -> 0 us
  between operations: 14.3 us -> 0.66 us
    gather x15 -> x0, local copies, waits for them, and re-layouts: 46.2 us -> none  [the longest x4 12.6 us: advance(): tally = jnp.sum(mask, axis=1) + jnp.take(tallies, keys)]
    psum x1 -> x0, waiting for transfers between devices: 39.8 us -> none  [carries(): closing_sums, closing_counts = lax.psum((slice_sums, slice_counts), 'tm')]
    pallas_call x0 -> x1, Pallas kernels: none -> 33.7 us  [local(): pl.pallas_call(functools.partial(kernel, na, nb, ng, count_parts, extra),...]
    all_gather x1 -> x0, blocking collectives: 27.5 us -> none  [carried_in(): everything = jax.tree.map(lambda part: lax.all_gather(part, axis), shard)]
    psum x1 -> x0, blocking collectives: 19.8 us -> none  [carries(): closing_sums, closing_counts = lax.psum((slice_sums, slice_counts), 'tm')]
    dot_general x8 -> x0, matrix products: 19.3 us -> none  [the longest x4 10.3 us: collect(): lax.dot_general(onehot, rows, (((0,), (0,)), ((), ())), precision=lax.Pre...]
    all_to_all x4 -> x0, starting transfers between devices: 14.2 us -> none  [the longest x1 4.23 us: carries(): lax.all_to_all(local_sums.reshape(owners, per_owner, width), 'group', spl...]
    all_to_all x4 -> x0, waiting for transfers between devices: 11.1 us -> none  [the longest x1 8.19 us: carries(): lax.all_to_all(local_sums.reshape(owners, per_owner, width), 'group', spl...]
  transfers between devices with their start and end apart: 6 -> 0, of which waited for: 3 -> 0; matrix products, arithmetic and copies ran while one was open for 27% -> 0% of each run, Pallas kernels for 0% -> 0%
where the time goes in v1:
time: 37.8 us; the launch traced here: 37.6 us
  Pallas kernels  33.7 us (89%)
  local copies, waits for them, and re-layouts  3.17 us (8%)
  between operations  0.66 us (2%)
    pallas_call x1, Pallas kernels, local(): pl.pallas_call(functools.partial(kernel, na, nb, ng, count_parts, extra),...  33.7 us
    unnamed x7, local copies, waits for them, and re-layouts  3.17 us

profile of v1, /device:TPU:0, one launch (start us, length us, event | category | flops | bytes accessed | tf_op | source)
XLA Modules:
  0.0 37.6 jit_solution(9173152122889946173)
XLA Ops:
  0.6 33.7 %running_totals.1 = (f32[64,2048]{1,0:T(8,128)}, s32[16,128]{1,0:T(8,128)}, f32[64,512]{1,0:T(8,128)}) custom-call(f32[64,2048]{1,0:T(8,128)} %bitcast.6, s32[16,128]{1,0:T(8,128)} %bitcast.9, s32[16,128]{1,0:T(8,128)} %bitcast.10), custom_call_target="tpu_custom_call" | custom-call | tf_op jit(solution)/shard_map/running_totals/pallas_call | solution.py:268
  34.4 0.0 copy-start.1
  34.4 0.0 copy-start
  34.4 1.9 %copy.9 = f32[2048,64]{0,1:T(8,128)} copy(f32[2048,64]{0,1:T(8,128)} %bitcast.7) | data formatting | bytes 1048576
  36.3 0.0 copy-done.1
  36.3 0.6 %copy.10 = s32[2048]{0:T(1024)} copy(s32[2048]{0:T(1024)S(1)} %bitcast.11) | data formatting | bytes 16384
  36.9 0.0 copy-done
  36.9 0.7 %copy.11 = f32[512,64]{0,1:T(8,128)} copy(f32[512,64]{0,1:T(8,128)S(1)} %bitcast.8) | data formatting | bytes 262144
Async XLA Ops:
  34.4 1.9 %copy-start.1 = (s32[16,128]{1,0:T(8,128)S(1)}, s32[16,128]{1,0:T(8,128)}, u32[]{:S(2)}) copy-start(s32[16,128]{1,0:T(8,128)} %get-tuple-element.7) | copy-start | bytes 24580
  34.4 2.5 %copy-start = (f32[64,512]{1,0:T(8,128)S(1)}, f32[64,512]{1,0:T(8,128)}, u32[]{:S(2)}) copy-start(f32[64,512]{1,0:T(8,128)} %get-tuple-element.8) | copy-start | bytes 393220

commit v2 on v1

v2 whole, which is shorter than its diff:
```python
import functools

import jax
import jax.numpy as jnp
from jax import lax
from jax.experimental import pallas as pl
from jax.experimental.pallas import tpu as pltpu
from jax.sharding import PartitionSpec as P

MESH = pl.DeviceIdType.MESH
LANES = 128
ROWS8 = 8
HALVES = 2
F32 = jnp.float32
BF16 = jnp.bfloat16


def split_parts(x, parts):
    pieces = []
    for _ in range(parts):
        piece = x.astype(BF16).astype(F32)
        pieces.append(piece)
        x = x - piece
    return pieces


def kernel(
    na, nb, ng, count_parts, extra,
    vt_ref, ids_ref, table_ref,
    mean_ref, count_ref, closing_ref,
    lhsv, onehot, cols, acc, lhss, mine, arrived, zbuf, back, start, shut,
    send1, recv1, sendz, recvz, send2, recv2, sendc, recvc,
):
    width, rows = vt_ref.shape
    groups = onehot.shape[0]
    plane = nb * ng
    per = groups // plane
    half = per // HALVES
    tm = lax.axis_index("tm")
    g_me = lax.axis_index("group")
    a_me, b_me = tm // nb, tm % nb
    p_me = b_me * ng + g_me
    o_me = g_me * nb + b_me

    def at_position(p):
        return (a_me * nb + p // ng, p % ng)

    def at_owner(o):
        return (a_me * nb + o % nb, o // nb)

    barrier = pltpu.get_barrier_semaphore()
    for k in range(1, plane):
        pl.semaphore_signal(
            barrier, inc=1, device_id=at_position((p_me + k) % plane), device_id_type=MESH
        )
    for k in range(1, na):
        pl.semaphore_signal(
            barrier, inc=1, device_id=(((a_me + k) % na) * nb + b_me, g_me), device_id_type=MESH
        )

    ids = ids_ref[...]
    low, high = ids & (LANES - 1), ids // LANES
    slots = []
    for i in range(0, ids.shape[0], ROWS8):
        index, page = low[i : i + ROWS8], high[i : i + ROWS8]
        found = jnp.zeros_like(index)
        for t in range(table_ref.shape[0]):
            entries = jnp.broadcast_to(table_ref[t : t + 1, :], index.shape)
            got = jnp.take_along_axis(entries, index, axis=1)
            found = jnp.where(page == t, got, found)
        slots.append(found)
    slots = jnp.concatenate(slots, axis=0)

    hi, lo = split_parts(vt_ref[...], 2)
    lhsv[0:width, :] = hi.astype(BF16)
    lhsv[width : 2 * width, :] = lo.astype(BF16)
    tail = jnp.where(lax.broadcasted_iota(jnp.int32, (extra, rows), 0) < ROWS8, 1.0, 0.0)
    lhsv[2 * width :, :] = tail.astype(BF16)

    turned = jnp.transpose(slots.astype(F32)).astype(jnp.int32)
    for b in range(rows // LANES):
        cols[b * LANES : (b + 1) * LANES, :] = jnp.broadcast_to(
            turned[:, b : b + 1], (LANES, LANES)
        )

    pl.semaphore_wait(barrier, plane - 1 + na - 1)

    def copy1(h, k, o, p):
        return pltpu.make_async_remote_copy(
            src_ref=mine.at[h, k],
            dst_ref=arrived.at[h, p],
            send_sem=send1.at[h, k],
            recv_sem=recv1.at[h, p],
            device_id=at_owner(o),
            device_id_type=MESH,
        )

    def copyz(h, k, a):
        return pltpu.make_async_remote_copy(
            src_ref=zbuf.at[h, a_me],
            dst_ref=zbuf.at[h, a],
            send_sem=sendz.at[h, k],
            recv_sem=recvz.at[h, a],
            device_id=(((a_me + k) % na) * nb + b_me, g_me),
            device_id_type=MESH,
        )

    def copy2(h, k, o):
        p = (p_me + k) % plane
        return pltpu.make_async_remote_copy(
            src_ref=back.at[h, p],
            dst_ref=start.at[h, o],
            send_sem=send2.at[h, k],
            recv_sem=recv2.at[h, o],
            device_id=at_position(p),
            device_id_type=MESH,
        )

    def copyc(h, k, b):
        return pltpu.make_async_remote_copy(
            src_ref=shut.at[h, b_me],
            dst_ref=shut.at[h, b],
            send_sem=sendc.at[h, k],
            recv_sem=recvc.at[h, b],
            device_id=(a_me * nb + (b_me + k) % nb, g_me),
            device_id_type=MESH,
        )

    order = [k % plane for k in range(1, plane + 1)]
    for h in range(HALVES):
        for first in range(0, plane, 2):
            pair = order[first : first + 2]
            masks = []
            for k in pair:
                label = lax.broadcasted_iota(jnp.int32, (1, half), 1)
                label = label + (((o_me + k) % plane) * per + h * half)
                masks.append(jnp.where(cols[:, 0:half] == label, 1.0, 0.0).astype(BF16))
            sums = jnp.dot(
                lhsv[...], jnp.concatenate(masks, axis=1), preferred_element_type=F32
            )
            for i, k in enumerate(pair):
                part = sums[:, i * half : (i + 1) * half]
                part = jnp.concatenate(
                    [
                        part[0:width] + part[width : 2 * width],
                        part[2 * width : 2 * width + ROWS8],
                    ],
                    axis=0,
                )
                if k:
                    mine[h, k] = part
                    copy1(h, k, (o_me + k) % plane, p_me).start()
                else:
                    arrived[h, p_me] = part

    def sum_plane(h):
        for k in range(1, plane):
            copy1(h, k, o_me, (p_me + plane - k) % plane).wait_recv()
        plane_sum = arrived[h, 0]
        for p in range(1, plane):
            plane_sum = plane_sum + arrived[h, p]
        zbuf[h, a_me] = plane_sum
        for k in range(1, na):
            copyz(h, k, a_me).start()

    def fill_onehot():
        for h in range(HALVES):
            for o in range(plane):
                base = (h * plane + o) * half
                labels = lax.broadcasted_iota(jnp.int32, (half, LANES), 0) + (o * per + h * half)
                for b in range(rows // LANES):
                    onehot[base : base + half, b * LANES : (b + 1) * LANES] = jnp.where(
                        labels == slots[b : b + 1, :], 1.0, 0.0
                    ).astype(BF16)

    def own_running():
        step = min(rows, 2 * LANES)
        for i in range(0, rows, step):
            column = cols[i : i + step, :]
            blocks = []
            for j in range(i, rows, LANES):
                hit = column == slots[j // LANES : j // LANES + 1, :]
                if j < i + step:
                    q = lax.broadcasted_iota(jnp.int32, (step, LANES), 0)
                    r = lax.broadcasted_iota(jnp.int32, (step, LANES), 1) + (j - i)
                    hit = hit & (q <= r)
                blocks.append(jnp.where(hit, 1.0, 0.0).astype(BF16))
            part = jnp.dot(
                lhsv[:, i : i + step], jnp.concatenate(blocks, axis=1), preferred_element_type=F32
            )
            if i == 0:
                acc[...] = part
            else:
                acc[:, i:] += part

    def send_back(h):
        for k in range(1, na):
            copyz(h, k, (a_me + na - k) % na).wait_recv()
        before = jnp.zeros((width + ROWS8, half), F32)
        for a in range(na):
            before = before + jnp.where(a < a_me, zbuf[h, a], 0.0)
        for p in range(plane):
            back[h, p] = before
            if p < plane - 1:
                before = before + arrived[h, p]
        for k in range(1, plane):
            copy2(h, k, o_me).start()
        start[h, o_me] = back[h, p_me]

    def close(h):
        total = zbuf[h, 0]
        for a in range(1, na):
            total = total + zbuf[h, a]
        shut[h, b_me] = total[0:width] * (1.0 / jnp.maximum(total[width : width + 1], 1.0))
        for k in range(1, nb):
            copyc(h, k, b_me).start()

    def take_start(h):
        for k in range(1, plane):
            copy2(h, k, (o_me + plane - k) % plane).wait_recv()
        for o in range(plane):
            one = start[h, o]
            counts = split_parts(one[width:], count_parts)
            pad = extra // ROWS8 - count_parts
            counts = counts + [jnp.zeros_like(counts[0])] * pad
            stacked = jnp.concatenate(split_parts(one[0:width], 2) + counts, axis=0)
            base = (h * plane + o) * half
            lhss[:, base : base + half] = stacked.astype(BF16)

    sum_plane(0)
    fill_onehot()
    for h in range(1, HALVES):
        sum_plane(h)
    own_running()
    for h in range(HALVES):
        send_back(h)
    for h in range(HALVES):
        close(h)

    wide = min(rows, 4 * LANES)
    deep = plane * half
    for h in range(HALVES):
        take_start(h)
        for i in range(0, rows, wide):
            whole = acc[:, i : i + wide] + jnp.dot(
                lhss[:, h * deep : (h + 1) * deep],
                onehot[h * deep : (h + 1) * deep, i : i + wide],
                preferred_element_type=F32,
            )
            if h < HALVES - 1:
                acc[:, i : i + wide] = whole
                continue
            count = whole[2 * width : 2 * width + 1]
            for j in range(1, count_parts):
                count = count + whole[2 * width + j * ROWS8 : 2 * width + j * ROWS8 + 1]
            mean_ref[:, i : i + wide] = (whole[0:width] + whole[width : 2 * width]) * (1.0 / count)
            count = count.astype(jnp.int32)
            for j in range(0, wide, LANES):
                b = (i + j) // LANES
                count_ref[b : b + 1, :] = count[:, j : j + LANES]

    for h in range(HALVES):
        for k in range(1, nb):
            copyc(h, k, (b_me + nb - k) % nb).wait_recv()
        for b in range(nb):
            at = b * per + h * half
            closing_ref[:, at : at + half] = shut[h, b]

    for h in range(HALVES):
        for k in range(1, plane):
            copy1(h, k, (o_me + k) % plane, p_me).wait_send()
            copy2(h, k, o_me).wait_send()
        for k in range(1, na):
            copyz(h, k, a_me).wait_send()
        for k in range(1, nb):
            copyc(h, k, b_me).wait_send()


def inner_parts(parts, owner_slots):
    best = 1
    for n in range(1, parts + 1):
        if n * n <= parts and parts % n == 0 and owner_slots % (n * HALVES * LANES) == 0:
            best = n
    return best


def solution(mesh):
    tm, ng = mesh.shape["tm"], mesh.shape["group"]

    def local(values, group_ids, slot_of):
        rows, width = values.shape
        groups = slot_of.shape[0]
        nb = inner_parts(tm, groups // ng)
        na = tm // nb
        plane = nb * ng
        half = groups // plane // HALVES
        count_parts = 2 if rows * tm * ng <= 2**17 else 3
        extra = 2 * ROWS8 if count_parts == 2 else 4 * ROWS8
        tall = 2 * width + extra
        sent = width + ROWS8
        vmem = pl.BlockSpec(memory_space=pltpu.VMEM)
        dma = pltpu.SemaphoreType.DMA
        mean, count, closing = pl.pallas_call(
            functools.partial(kernel, na, nb, ng, count_parts, extra),
            out_shape=(
                jax.ShapeDtypeStruct((width, rows), F32),
                jax.ShapeDtypeStruct((rows // LANES, LANES), jnp.int32),
                jax.ShapeDtypeStruct((width, groups // ng), F32),
            ),
            in_specs=[vmem] * 3,
            out_specs=(vmem,) * 3,
            scratch_shapes=[
                pltpu.VMEM((tall, rows), BF16),
                pltpu.VMEM((groups, rows), BF16),
                pltpu.VMEM((rows, LANES), jnp.int32),
                pltpu.VMEM((tall, rows), F32),
                pltpu.VMEM((tall, groups), BF16),
                pltpu.VMEM((HALVES, plane, sent, half), F32),
                pltpu.VMEM((HALVES, plane, sent, half), F32),
                pltpu.VMEM((HALVES, na, sent, half), F32),
                pltpu.VMEM((HALVES, plane, sent, half), F32),
                pltpu.VMEM((HALVES, plane, sent, half), F32),
                pltpu.VMEM((HALVES, nb, width, half), F32),
                dma((HALVES, plane)), dma((HALVES, plane)), dma((HALVES, na)), dma((HALVES, na)),
                dma((HALVES, plane)), dma((HALVES, plane)), dma((HALVES, nb)), dma((HALVES, nb)),
            ],
            compiler_params=pltpu.CompilerParams(
                collective_id=0, has_side_effects=True, vmem_limit_bytes=60 * 1024 * 1024
            ),
            name="running_totals",
        )(
            values.T,
            group_ids.reshape(rows // LANES, LANES),
            slot_of.reshape(groups // LANES, LANES),
        )
        return mean.T, count.reshape(rows), closing.T

    in_specs = (P(("tm", "group"), None), P(("tm", "group")), P())
    out_specs = (P(("tm", "group"), None), P(("tm", "group")), P("group", None))
    return jax.shard_map(local, mesh=mesh, in_specs=in_specs, out_specs=out_specs, check_vma=False)
```

time: 37.8 us -> 31.9 us (0.84)
  Pallas kernels: 33.7 us -> 27.9 us
    pallas_call x1, Pallas kernels: 33.7 us -> 27.9 us  [local(): pl.pallas_call(functools.partial(kernel, na, nb, ng, count_parts, extra),...]
where the time goes in v2:
time: 31.9 us; the launch traced here: 31.7 us
  Pallas kernels  27.9 us (87%)
  local copies, waits for them, and re-layouts  3.17 us (10%)
  between operations  0.66 us (2%)
    pallas_call x1, Pallas kernels, local(): pl.pallas_call(functools.partial(kernel, na, nb, ng, count_parts, extra),...  27.9 us
    unnamed x7, local copies, waits for them, and re-layouts  3.17 us

profile of v2, /device:TPU:0, one launch (start us, length us, event | category | flops | bytes accessed | tf_op | source)
XLA Modules:
  0.0 31.7 jit_solution(12841099115387056569)
XLA Ops:
  0.6 27.9 %running_totals.1 = (f32[64,2048]{1,0:T(8,128)}, s32[16,128]{1,0:T(8,128)}, f32[64,512]{1,0:T(8,128)}) custom-call(f32[64,2048]{1,0:T(8,128)} %bitcast.6, s32[16,128]{1,0:T(8,128)} %bitcast.9, s32[16,128]{1,0:T(8,128)} %bitcast.10), custom_call_target="tpu_custom_call" | custom-call | tf_op jit(solution)/shard_map/running_totals/pallas_call | solution.py:303
  28.6 0.0 copy-start.1
  28.6 0.0 copy-start
  28.6 1.9 %copy.9 = f32[2048,64]{0,1:T(8,128)} copy(f32[2048,64]{0,1:T(8,128)} %bitcast.7) | data formatting | bytes 1048576
  30.5 0.0 copy-done.1
  30.5 0.6 %copy.10 = s32[2048]{0:T(1024)} copy(s32[2048]{0:T(1024)S(1)} %bitcast.11) | data formatting | bytes 16384
  31.1 0.0 copy-done
  31.1 0.7 %copy.11 = f32[512,64]{0,1:T(8,128)} copy(f32[512,64]{0,1:T(8,128)S(1)} %bitcast.8) | data formatting | bytes 262144
Async XLA Ops:
  28.6 1.9 %copy-start.1 = (s32[16,128]{1,0:T(8,128)S(1)}, s32[16,128]{1,0:T(8,128)}, u32[]{:S(2)}) copy-start(s32[16,128]{1,0:T(8,128)} %get-tuple-element.7) | copy-start | bytes 24580
  28.6 2.5 %copy-start = (f32[64,512]{1,0:T(8,128)S(1)}, f32[64,512]{1,0:T(8,128)}, u32[]{:S(2)}) copy-start(f32[64,512]{1,0:T(8,128)} %get-tuple-element.8) | copy-start | bytes 393220

commit v3 on v2

--- a/solution.py
+++ b/solution.py
@@ -28,30 +28,38 @@
     na, nb, ng, count_parts, extra,
     vt_ref, ids_ref, table_ref,
     mean_ref, count_ref, closing_ref,
-    lhsv, onehot, cols, acc, lhss, mine, arrived, zbuf, back, start, shut,
-    send1, recv1, sendz, recvz, send2, recv2, sendc, recvc,
+    lhsv, onehot, cols, acc, lhss, give, got, own, mine, arrived, zbuf, back, start, onward, came,
+    shut, sendd, recvd, sendf, recvf, send1, recv1, sendz, recvz, send2, recv2, sendc, recvc,
 ):
     width, rows = vt_ref.shape
     groups = onehot.shape[0]
-    plane = nb * ng
-    per = groups // plane
+    nx = ng // 2
+    pairs = nb * nx
+    per = groups // (2 * pairs)
     half = per // HALVES
     tm = lax.axis_index("tm")
     g_me = lax.axis_index("group")
     a_me, b_me = tm // nb, tm % nb
-    p_me = b_me * ng + g_me
-    o_me = g_me * nb + b_me
+    x_me, c_me = g_me // 2, g_me % 2
+    c_other = 1 - c_me
+    p_me = b_me * nx + x_me
+    o_me = x_me * nb + b_me
 
     def at_position(p):
-        return (a_me * nb + p // ng, p % ng)
+        return (a_me * nb + p // nx, 2 * (p % nx) + c_me)
 
     def at_owner(o):
-        return (a_me * nb + o % nb, o // nb)
-
+        return (a_me * nb + o % nb, 2 * (o // nb) + c_me)
+
+    def first_slot(o, c, h):
+        return ((2 * (o // nb) + c) * nb + o % nb) * per + h * half
+
+    partner = (tm, 2 * x_me + c_other)
     barrier = pltpu.get_barrier_semaphore()
-    for k in range(1, plane):
+    pl.semaphore_signal(barrier, inc=1, device_id=partner, device_id_type=MESH)
+    for k in range(1, pairs):
         pl.semaphore_signal(
-            barrier, inc=1, device_id=at_position((p_me + k) % plane), device_id_type=MESH
+            barrier, inc=1, device_id=at_position((p_me + k) % pairs), device_id_type=MESH
         )
     for k in range(1, na):
         pl.semaphore_signal(
@@ -66,8 +74,8 @@
         found = jnp.zeros_like(index)
         for t in range(table_ref.shape[0]):
             entries = jnp.broadcast_to(table_ref[t : t + 1, :], index.shape)
-            got = jnp.take_along_axis(entries, index, axis=1)
-            found = jnp.where(page == t, got, found)
+            hit = jnp.take_along_axis(entries, index, axis=1)
+            found = jnp.where(page == t, hit, found)
         slots.append(found)
     slots = jnp.concatenate(slots, axis=0)
 
@@ -83,11 +91,31 @@
             turned[:, b : b + 1], (LANES, LANES)
         )
 
-    pl.semaphore_wait(barrier, plane - 1 + na - 1)
+    pl.semaphore_wait(barrier, pairs + na - 1)
+
+    def copyd(h):
+        return pltpu.make_async_remote_copy(
+            src_ref=give.at[h],
+            dst_ref=got.at[h],
+            send_sem=sendd.at[h],
+            recv_sem=recvd.at[h],
+            device_id=partner,
+            device_id_type=MESH,
+        )
+
+    def copyf(h):
+        return pltpu.make_async_remote_copy(
+            src_ref=onward.at[h],
+            dst_ref=came.at[h],
+            send_sem=sendf.at[h],
+            recv_sem=recvf.at[h],
+            device_id=partner,
+            device_id_type=MESH,
+        )
 
     def copy1(h, k, o, p):
         return pltpu.make_async_remote_copy(
-            src_ref=mine.at[h, k],
+            src_ref=mine.at[h, o],
             dst_ref=arrived.at[h, p],
             send_sem=send1.at[h, k],
             recv_sem=recv1.at[h, p],
@@ -106,7 +134,7 @@
         )
 
     def copy2(h, k, o):
-        p = (p_me + k) % plane
+        p = (p_me + k) % pairs
         return pltpu.make_async_remote_copy(
             src_ref=back.at[h, p],
             dst_ref=start.at[h, o],
@@ -126,38 +154,39 @@
             device_id_type=MESH,
         )
 
-    order = [k % plane for k in range(1, plane + 1)]
-    for h in range(HALVES):
-        for first in range(0, plane, 2):
-            pair = order[first : first + 2]
+    def slot_sums(h, c, into):
+        for first in range(0, pairs, 2):
+            two = range(first, min(first + 2, pairs))
             masks = []
-            for k in pair:
-                label = lax.broadcasted_iota(jnp.int32, (1, half), 1)
-                label = label + (((o_me + k) % plane) * per + h * half)
+            for o in two:
+                label = lax.broadcasted_iota(jnp.int32, (1, half), 1) + first_slot(o, c, h)
                 masks.append(jnp.where(cols[:, 0:half] == label, 1.0, 0.0).astype(BF16))
             sums = jnp.dot(
                 lhsv[...], jnp.concatenate(masks, axis=1), preferred_element_type=F32
             )
-            for i, k in enumerate(pair):
+            for i, o in enumerate(two):
                 part = sums[:, i * half : (i + 1) * half]
-                part = jnp.concatenate(
+                into[h, o] = jnp.concatenate(
                     [
                         part[0:width] + part[width : 2 * width],
                         part[2 * width : 2 * width + ROWS8],
                     ],
                     axis=0,
                 )
-                if k:
-                    mine[h, k] = part
-                    copy1(h, k, (o_me + k) % plane, p_me).start()
-                else:
-                    arrived[h, p_me] = part
+
+    def send_pair_sums(h):
+        copyd(h).wait_recv()
+        for o in range(pairs):
+            mine[h, o] = own[h, o] + got[h, o]
+        for k in range(1, pairs):
+            copy1(h, k, (o_me + k) % pairs, p_me).start()
+        arrived[h, p_me] = mine[h, o_me]
 
     def sum_plane(h):
-        for k in range(1, plane):
-            copy1(h, k, o_me, (p_me + plane - k) % plane).wait_recv()
+        for k in range(1, pairs):
+            copy1(h, k, o_me, (p_me + pairs - k) % pairs).wait_recv()
         plane_sum = arrived[h, 0]
-        for p in range(1, plane):
+        for p in range(1, pairs):
             plane_sum = plane_sum + arrived[h, p]
         zbuf[h, a_me] = plane_sum
         for k in range(1, na):
@@ -165,13 +194,14 @@
 
     def fill_onehot():
         for h in range(HALVES):
-            for o in range(plane):
-                base = (h * plane + o) * half
-                labels = lax.broadcasted_iota(jnp.int32, (half, LANES), 0) + (o * per + h * half)
-                for b in range(rows // LANES):
-                    onehot[base : base + half, b * LANES : (b + 1) * LANES] = jnp.where(
-                        labels == slots[b : b + 1, :], 1.0, 0.0
-                    ).astype(BF16)
+            for i, c in enumerate((c_me, c_other)):
+                for o in range(pairs):
+                    base = ((h * 2 + i) * pairs + o) * half
+                    labels = lax.broadcasted_iota(jnp.int32, (half, LANES), 0) + first_slot(o, c, h)
+                    for b in range(rows // LANES):
+                        onehot[base : base + half, b * LANES : (b + 1) * LANES] = jnp.where(
+                            labels == slots[b : b + 1, :], 1.0, 0.0
+                        ).astype(BF16)
 
     def own_running():
         step = min(rows, 2 * LANES)
@@ -199,11 +229,11 @@
         before = jnp.zeros((width + ROWS8, half), F32)
         for a in range(na):
             before = before + jnp.where(a < a_me, zbuf[h, a], 0.0)
-        for p in range(plane):
+        for p in range(pairs):
             back[h, p] = before
-            if p < plane - 1:
+            if p < pairs - 1:
                 before = before + arrived[h, p]
-        for k in range(1, plane):
+        for k in range(1, pairs):
             copy2(h, k, o_me).start()
         start[h, o_me] = back[h, p_me]
 
@@ -215,39 +245,38 @@
         for k in range(1, nb):
             copyc(h, k, b_me).start()
 
+    def set_start(one, at):
+        counts = split_parts(one[width:], count_parts)
+        pad = extra // ROWS8 - count_parts
+        counts = counts + [jnp.zeros_like(counts[0])] * pad
+        stacked = jnp.concatenate(split_parts(one[0:width], 2) + counts, axis=0)
+        lhss[:, at * half : (at + 1) * half] = stacked.astype(BF16)
+
     def take_start(h):
-        for k in range(1, plane):
-            copy2(h, k, (o_me + plane - k) % plane).wait_recv()
-        for o in range(plane):
-            one = start[h, o]
-            counts = split_parts(one[width:], count_parts)
-            pad = extra // ROWS8 - count_parts
-            counts = counts + [jnp.zeros_like(counts[0])] * pad
-            stacked = jnp.concatenate(split_parts(one[0:width], 2) + counts, axis=0)
-            base = (h * plane + o) * half
-            lhss[:, base : base + half] = stacked.astype(BF16)
-
-    sum_plane(0)
-    fill_onehot()
-    for h in range(1, HALVES):
-        sum_plane(h)
-    own_running()
-    for h in range(HALVES):
-        send_back(h)
-    for h in range(HALVES):
-        close(h)
+        for k in range(1, pairs):
+            copy2(h, k, (o_me + pairs - k) % pairs).wait_recv()
+        for o in range(pairs):
+            onward[h, o] = start[h, o] + jnp.where(c_me == 0, own[h, o], 0.0)
+        copyf(h).start()
+        for o in range(pairs):
+            set_start(start[h, o] + jnp.where(c_me == 1, got[h, o], 0.0), h * 2 * pairs + o)
+
+    def take_other(h):
+        copyf(h).wait_recv()
+        for o in range(pairs):
+            set_start(came[h, o], (h * 2 + 1) * pairs + o)
 
     wide = min(rows, 4 * LANES)
-    deep = plane * half
-    for h in range(HALVES):
-        take_start(h)
+    deep = pairs * half
+
+    def add_start(block, last):
         for i in range(0, rows, wide):
             whole = acc[:, i : i + wide] + jnp.dot(
-                lhss[:, h * deep : (h + 1) * deep],
-                onehot[h * deep : (h + 1) * deep, i : i + wide],
+                lhss[:, block * deep : (block + 1) * deep],
+                onehot[block * deep : (block + 1) * deep, i : i + wide],
                 preferred_element_type=F32,
             )
-            if h < HALVES - 1:
+            if not last:
                 acc[:, i : i + wide] = whole
                 continue
             count = whole[2 * width : 2 * width + 1]
@@ -259,6 +288,30 @@
                 b = (i + j) // LANES
                 count_ref[b : b + 1, :] = count[:, j : j + LANES]
 
+    slot_sums(0, c_other, give)
+    copyd(0).start()
+    slot_sums(0, c_me, own)
+    for h in range(1, HALVES):
+        slot_sums(h, c_other, give)
+        copyd(h).start()
+        send_pair_sums(h - 1)
+        slot_sums(h, c_me, own)
+    send_pair_sums(HALVES - 1)
+    sum_plane(0)
+    fill_onehot()
+    for h in range(1, HALVES):
+        sum_plane(h)
+    own_running()
+    for h in range(HALVES):
+        send_back(h)
+    for h in range(HALVES):
+        close(h)
+    for h in range(HALVES):
+        take_start(h)
+        add_start(2 * h, False)
+        take_other(h)
+        add_start(2 * h + 1, h == HALVES - 1)
+
     for h in range(HALVES):
         for k in range(1, nb):
             copyc(h, k, (b_me + nb - k) % nb).wait_recv()
@@ -267,8 +320,10 @@
             closing_ref[:, at : at + half] = shut[h, b]
 
     for h in range(HALVES):
-        for k in range(1, plane):
-            copy1(h, k, (o_me + k) % plane, p_me).wait_send()
+        copyd(h).wait_send()
+        copyf(h).wait_send()
+        for k in range(1, pairs):
+            copy1(h, k, (o_me + k) % pairs, p_me).wait_send()
             copy2(h, k, o_me).wait_send()
         for k in range(1, na):
             copyz(h, k, a_me).wait_send()
@@ -292,8 +347,8 @@
         groups = slot_of.shape[0]
         nb = inner_parts(tm, groups // ng)
         na = tm // nb
-        plane = nb * ng
-        half = groups // plane // HALVES
+        pairs = nb * ng // 2
+        half = groups // (2 * pairs) // HALVES
         count_parts = 2 if rows * tm * ng <= 2**17 else 3
         extra = 2 * ROWS8 if count_parts == 2 else 4 * ROWS8
         tall = 2 * width + extra
@@ -315,14 +370,20 @@
                 pltpu.VMEM((rows, LANES), jnp.int32),
                 pltpu.VMEM((tall, rows), F32),
                 pltpu.VMEM((tall, groups), BF16),
-                pltpu.VMEM((HALVES, plane, sent, half), F32),
-                pltpu.VMEM((HALVES, plane, sent, half), F32),
+                pltpu.VMEM((HALVES, pairs, sent, half), F32),
+                pltpu.VMEM((HALVES, pairs, sent, half), F32),
+                pltpu.VMEM((HALVES, pairs, sent, half), F32),
+                pltpu.VMEM((HALVES, pairs, sent, half), F32),
+                pltpu.VMEM((HALVES, pairs, sent, half), F32),
                 pltpu.VMEM((HALVES, na, sent, half), F32),
-                pltpu.VMEM((HALVES, plane, sent, half), F32),
-                pltpu.VMEM((HALVES, plane, sent, half), F32),
+                pltpu.VMEM((HALVES, pairs, sent, half), F32),
+                pltpu.VMEM((HALVES, pairs, sent, half), F32),
+                pltpu.VMEM((HALVES, pairs, sent, half), F32),
+                pltpu.VMEM((HALVES, pairs, sent, half), F32),
                 pltpu.VMEM((HALVES, nb, width, half), F32),
-                dma((HALVES, plane)), dma((HALVES, plane)), dma((HALVES, na)), dma((HALVES, na)),
-                dma((HALVES, plane)), dma((HALVES, plane)), dma((HALVES, nb)), dma((HALVES, nb)),
+                dma((HALVES,)), dma((HALVES,)), dma((HALVES,)), dma((HALVES,)),
+                dma((HALVES, pairs)), dma((HALVES, pairs)), dma((HALVES, na)), dma((HALVES, na)),
+                dma((HALVES, pairs)), dma((HALVES, pairs)), dma((HALVES, nb)), dma((HALVES, nb)),
             ],
             compiler_params=pltpu.CompilerParams(
                 collective_id=0, has_side_effects=True, vmem_limit_bytes=60 * 1024 * 1024

time: 31.9 us -> 30.8 us (0.966); the launches traced: 31.7 us -> 30.3 us
  Pallas kernels: 27.9 us -> 26.4 us
    pallas_call x1, Pallas kernels: 27.9 us -> 26.4 us  [local(): pl.pallas_call(functools.partial(kernel, na, nb, ng, count_parts, extra),...]
where the time goes in v3:
time: 30.8 us; the launch traced here: 30.3 us
  Pallas kernels  26.4 us (86%)
  local copies, waits for them, and re-layouts  3.17 us (10%)
  between operations  0.66 us (2%)
    pallas_call x1, Pallas kernels, local(): pl.pallas_call(functools.partial(kernel, na, nb, ng, count_parts, extra),...  26.4 us
    unnamed x7, local copies, waits for them, and re-layouts  3.17 us

profile of v3, /device:TPU:0, one launch (start us, length us, event | category | flops | bytes accessed | tf_op | source)
XLA Modules:
  0.0 30.3 jit_solution(16732893083481674258)
XLA Ops:
  0.6 26.4 %running_totals.1 = (f32[64,2048]{1,0:T(8,128)}, s32[16,128]{1,0:T(8,128)}, f32[64,512]{1,0:T(8,128)}) custom-call(f32[64,2048]{1,0:T(8,128)} %bitcast.6, s32[16,128]{1,0:T(8,128)} %bitcast.9, s32[16,128]{1,0:T(8,128)} %bitcast.10), custom_call_target="tpu_custom_call" | custom-call | tf_op jit(solution)/shard_map/running_totals/pallas_call | solution.py:358
  27.1 0.0 copy-start.1
  27.1 0.0 copy-start
  27.1 1.9 %copy.9 = f32[2048,64]{0,1:T(8,128)} copy(f32[2048,64]{0,1:T(8,128)} %bitcast.7) | data formatting | bytes 1048576
  29.0 0.0 copy-done.1
  29.0 0.6 %copy.10 = s32[2048]{0:T(1024)} copy(s32[2048]{0:T(1024)S(1)} %bitcast.11) | data formatting | bytes 16384
  29.6 0.0 copy-done
  29.6 0.7 %copy.11 = f32[512,64]{0,1:T(8,128)} copy(f32[512,64]{0,1:T(8,128)S(1)} %bitcast.8) | data formatting | bytes 262144
Async XLA Ops:
  27.1 1.9 %copy-start.1 = (s32[16,128]{1,0:T(8,128)S(1)}, s32[16,128]{1,0:T(8,128)}, u32[]{:S(2)}) copy-start(s32[16,128]{1,0:T(8,128)} %get-tuple-element.7) | copy-start | bytes 24580
  27.1 2.5 %copy-start = (f32[64,512]{1,0:T(8,128)S(1)}, f32[64,512]{1,0:T(8,128)}, u32[]{:S(2)}) copy-start(f32[64,512]{1,0:T(8,128)} %get-tuple-element.8) | copy-start | bytes 393220

commit v4 on v3

--- a/solution.py
+++ b/solution.py
@@ -28,7 +28,7 @@
     na, nb, ng, count_parts, extra,
     vt_ref, ids_ref, table_ref,
     mean_ref, count_ref, closing_ref,
-    lhsv, onehot, cols, acc, lhss, give, got, own, mine, arrived, zbuf, back, start, onward, came,
+    lhsv, onehot, cols, acc, lhss, give, got, own, mine, arrived, zbuf, zgot, back, start, onward, came,
     shut, sendd, recvd, sendf, recvf, send1, recv1, sendz, recvz, send2, recv2, sendc, recvc,
 ):
     width, rows = vt_ref.shape
@@ -55,16 +55,20 @@
         return ((2 * (o // nb) + c) * nb + o % nb) * per + h * half
 
     partner = (tm, 2 * x_me + c_other)
+    levels = na.bit_length() - 1
+
+    def across(t):
+        upper = (a_me // 2**t) % 2
+        return ((a_me + 2**t * (1 - 2 * upper)) * nb + b_me, g_me)
+
     barrier = pltpu.get_barrier_semaphore()
     pl.semaphore_signal(barrier, inc=1, device_id=partner, device_id_type=MESH)
     for k in range(1, pairs):
         pl.semaphore_signal(
             barrier, inc=1, device_id=at_position((p_me + k) % pairs), device_id_type=MESH
         )
-    for k in range(1, na):
-        pl.semaphore_signal(
-            barrier, inc=1, device_id=(((a_me + k) % na) * nb + b_me, g_me), device_id_type=MESH
-        )
+    for t in range(levels):
+        pl.semaphore_signal(barrier, inc=1, device_id=across(t), device_id_type=MESH)
 
     ids = ids_ref[...]
     low, high = ids & (LANES - 1), ids // LANES
@@ -91,7 +95,7 @@
             turned[:, b : b + 1], (LANES, LANES)
         )
 
-    pl.semaphore_wait(barrier, pairs + na - 1)
+    pl.semaphore_wait(barrier, pairs + levels)
 
     def copyd(h):
         return pltpu.make_async_remote_copy(
@@ -123,13 +127,13 @@
             device_id_type=MESH,
         )
 
-    def copyz(h, k, a):
-        return pltpu.make_async_remote_copy(
-            src_ref=zbuf.at[h, a_me],
-            dst_ref=zbuf.at[h, a],
-            send_sem=sendz.at[h, k],
-            recv_sem=recvz.at[h, a],
-            device_id=(((a_me + k) % na) * nb + b_me, g_me),
+    def copyz(h, t):
+        return pltpu.make_async_remote_copy(
+            src_ref=zbuf.at[h, t],
+            dst_ref=zgot.at[h, t],
+            send_sem=sendz.at[h, t],
+            recv_sem=recvz.at[h, t],
+            device_id=across(t),
             device_id_type=MESH,
         )
 
@@ -188,9 +192,15 @@
         plane_sum = arrived[h, 0]
         for p in range(1, pairs):
             plane_sum = plane_sum + arrived[h, p]
-        zbuf[h, a_me] = plane_sum
-        for k in range(1, na):
-            copyz(h, k, a_me).start()
+        zbuf[h, 0] = plane_sum
+        if levels:
+            copyz(h, 0).start()
+
+    def double(h, t):
+        copyz(h, t).wait_recv()
+        zbuf[h, t + 1] = zbuf[h, t] + zgot[h, t]
+        if t + 1 < levels:
+            copyz(h, t + 1).start()
 
     def fill_onehot():
         for h in range(HALVES):
@@ -224,11 +234,11 @@
                 acc[:, i:] += part
 
     def send_back(h):
-        for k in range(1, na):
-            copyz(h, k, (a_me + na - k) % na).wait_recv()
+        for t in range(1, levels):
+            double(h, t)
         before = jnp.zeros((width + ROWS8, half), F32)
-        for a in range(na):
-            before = before + jnp.where(a < a_me, zbuf[h, a], 0.0)
+        for t in range(levels):
+            before = before + jnp.where((a_me // 2**t) % 2 == 1, zgot[h, t], 0.0)
         for p in range(pairs):
             back[h, p] = before
             if p < pairs - 1:
@@ -238,9 +248,7 @@
         start[h, o_me] = back[h, p_me]
 
     def close(h):
-        total = zbuf[h, 0]
-        for a in range(1, na):
-            total = total + zbuf[h, a]
+        total = zbuf[h, levels]
         shut[h, b_me] = total[0:width] * (1.0 / jnp.maximum(total[width : width + 1], 1.0))
         for k in range(1, nb):
             copyc(h, k, b_me).start()
@@ -301,7 +309,11 @@
     fill_onehot()
     for h in range(1, HALVES):
         sum_plane(h)
+        if levels:
+            double(h - 1, 0)
     own_running()
+    if levels:
+        double(HALVES - 1, 0)
     for h in range(HALVES):
         send_back(h)
     for h in range(HALVES):
@@ -325,8 +337,8 @@
         for k in range(1, pairs):
             copy1(h, k, (o_me + k) % pairs, p_me).wait_send()
             copy2(h, k, o_me).wait_send()
-        for k in range(1, na):
-            copyz(h, k, a_me).wait_send()
+        for t in range(levels):
+            copyz(h, t).wait_send()
         for k in range(1, nb):
             copyc(h, k, b_me).wait_send()
 
@@ -347,6 +359,8 @@
         groups = slot_of.shape[0]
         nb = inner_parts(tm, groups // ng)
         na = tm // nb
+        assert na & (na - 1) == 0
+        steps = na.bit_length() - 1
         pairs = nb * ng // 2
         half = groups // (2 * pairs) // HALVES
         count_parts = 2 if rows * tm * ng <= 2**17 else 3
@@ -375,14 +389,15 @@
                 pltpu.VMEM((HALVES, pairs, sent, half), F32),
                 pltpu.VMEM((HALVES, pairs, sent, half), F32),
                 pltpu.VMEM((HALVES, pairs, sent, half), F32),
-                pltpu.VMEM((HALVES, na, sent, half), F32),
+                pltpu.VMEM((HALVES, steps + 1, sent, half), F32),
+                pltpu.VMEM((HALVES, max(steps, 1), sent, half), F32),
                 pltpu.VMEM((HALVES, pairs, sent, half), F32),
                 pltpu.VMEM((HALVES, pairs, sent, half), F32),
                 pltpu.VMEM((HALVES, pairs, sent, half), F32),
                 pltpu.VMEM((HALVES, pairs, sent, half), F32),
                 pltpu.VMEM((HALVES, nb, width, half), F32),
                 dma((HALVES,)), dma((HALVES,)), dma((HALVES,)), dma((HALVES,)),
-                dma((HALVES, pairs)), dma((HALVES, pairs)), dma((HALVES, na)), dma((HALVES, na)),
+                dma((HALVES, pairs)), dma((HALVES, pairs)), dma((HALVES, max(steps, 1))), dma((HALVES, max(steps, 1))),
                 dma((HALVES, pairs)), dma((HALVES, pairs)), dma((HALVES, nb)), dma((HALVES, nb)),
             ],
             compiler_params=pltpu.CompilerParams(

time: 30.8 us -> 33.2 us (1.078); the launches traced: 30.3 us -> 33 us
  Pallas kernels: 26.4 us -> 29.2 us
    pallas_call x1, Pallas kernels: 26.4 us -> 29.2 us  [local(): pl.pallas_call(functools.partial(kernel, na, nb, ng, count_parts, extra),...]
where the time goes in v4:
time: 33.2 us; the launch traced here: 33 us
  Pallas kernels  29.2 us (88%)
  local copies, waits for them, and re-layouts  3.17 us (10%)
  between operations  0.66 us (2%)
    pallas_call x1, Pallas kernels, local(): pl.pallas_call(functools.partial(kernel, na, nb, ng, count_parts, extra),...  29.2 us
    unnamed x7, local copies, waits for them, and re-layouts  3.17 us

profile of v4, /device:TPU:0, one launch (start us, length us, event | category | flops | bytes accessed | tf_op | source)
XLA Modules:
  0.0 33.0 jit_solution(7897152989667730612)
XLA Ops:
  0.6 29.2 %running_totals.1 = (f32[64,2048]{1,0:T(8,128)}, s32[16,128]{1,0:T(8,128)}, f32[64,512]{1,0:T(8,128)}) custom-call(f32[64,2048]{1,0:T(8,128)} %bitcast.6, s32[16,128]{1,0:T(8,128)} %bitcast.9, s32[16,128]{1,0:T(8,128)} %bitcast.10), custom_call_target="tpu_custom_call" | custom-call | tf_op jit(solution)/shard_map/running_totals/pallas_call | solution.py:372
  29.8 0.0 copy-start.1
  29.8 0.0 copy-start
  29.8 1.9 %copy.9 = f32[2048,64]{0,1:T(8,128)} copy(f32[2048,64]{0,1:T(8,128)} %bitcast.7) | data formatting | bytes 1048576
  31.7 0.0 copy-done.1
  31.8 0.6 %copy.10 = s32[2048]{0:T(1024)} copy(s32[2048]{0:T(1024)S(1)} %bitcast.11) | data formatting | bytes 16384
  32.4 0.0 copy-done
  32.4 0.7 %copy.11 = f32[512,64]{0,1:T(8,128)} copy(f32[512,64]{0,1:T(8,128)S(1)} %bitcast.8) | data formatting | bytes 262144
Async XLA Ops:
  29.8 1.9 %copy-start.1 = (s32[16,128]{1,0:T(8,128)S(1)}, s32[16,128]{1,0:T(8,128)}, u32[]{:S(2)}) copy-start(s32[16,128]{1,0:T(8,128)} %get-tuple-element.7) | copy-start | bytes 24580
  29.8 2.5 %copy-start = (f32[64,512]{1,0:T(8,128)S(1)}, f32[64,512]{1,0:T(8,128)}, u32[]{:S(2)}) copy-start(f32[64,512]{1,0:T(8,128)} %get-tuple-element.8) | copy-start | bytes 393220
